TPU v7x, 32 devices: a whole 2x2x4 slice. The times are simulated.
32 devices in a mesh: grp: 8 (over z, x), tp: 4 (over y, core).
Axes of the slice: x: 2, y: 2, z: 4, core: 2. Of those that a mesh axis runs over, the one named last changes fastest.
Arguments:
- q_nope: bfloat16 [512, 16384], P('grp', 'tp'), may hold values from -6 to 6
- q_rope: bfloat16 [512, 8192], P('grp', 'tp'), may hold values from -500 to 500
- w_uk: bfloat16 [128, 128, 512], P('tp'), may hold values from -0.5 to 0.5
- w_uv: bfloat16 [128, 512, 128], P('tp'), may hold values from -1 to 1
- prefix_latent: bfloat16 [16, 2048, 512], P('grp'), may hold values from -5 to 5
- prefix_rope: bfloat16 [16, 64, 2048], P('grp'), may hold values from -8 to 8
- suffix_latent: bfloat16 [512, 256, 512], P(('grp', 'tp')), may hold values from -5 to 5
- suffix_rope: bfloat16 [512, 64, 256], P(('grp', 'tp')), may hold values from -4 to 4
- suffix_len: int32 [8, 64], P('grp'), may hold values from 1 to 256, 8192 in all within a row
- request_prefix: int32 [512], P('grp'), may hold values from 0 to 15, as said below
- prefix_slot: int32 [16], replicated, may hold values from 0 to 15, as said below
Outputs:
- attended: bfloat16 [512, 16384], P('grp', 'tp')
Inputs may be any that keep to these rules, and one draw needn't show every extreme that they name: `request_prefix`: of the requests of one group, at most 8 name the same prefix; in every draw one prefix is named by exactly 8 requests of every group. `prefix_slot`: A permutation: each cache row holds exactly one prefix. `suffix_len`: the lengths of one group sum to 8192, and one of them is 256.
All inputs are finite; a program needn't handle non-finite values.
Results may differ from a plain program's by a relative error of at most 0.018.
Values may be sent and summed in bfloat16 or wider, within the bound.
A program may use at most 128 MiB of HBM per device.

v0:
```python
import functools
import math

import jax
import jax.numpy as jnp
from jax import lax
from jax.experimental import pallas as pl
from jax.experimental.pallas import tpu as pltpu
from jax.sharding import PartitionSpec as P

MESH = pl.DeviceIdType.MESH
CHUNKS = 4
SPLIT = 2
F32 = jnp.float32
BF16 = jnp.bfloat16


def mm(a, b):
    return jnp.dot(a, b, preferred_element_type=F32)


def mm_t(a, b):
    return lax.dot_general(a, b, (((1,), (1,)), ((), ())), preferred_element_type=F32)


def kernel(dims, *refs):
    n, t, chunks, cap, score_scale = dims
    (q_nope, q_rope, placing, sending, perm, perm_t, sel, sel_t, lens) = refs[:9]
    hbm = refs[9:15]
    out = refs[15]
    held = refs[16:22]
    wuk, wuv, plat, prope, slat, srope = held
    (qs, qr, qh, tqs, tqr, tropes, rq, sos, sor, ssts, sstr, vbs, vbr, st, sts, strv, vall, svals) = refs[22:40]
    (load_sem, rope_ss, rope_rs, tq_ss, tq_rs, so_ss, so_rs, sst_ss, sst_rs, q_ss, q_rs, vb_ss, vb_rs, st_ss, st_rs) = refs[40:]
    g = lax.axis_index("grp")
    y = lax.axis_index("tp")
    batch = q_nope.shape[0]
    heads, nope, latent = wuk.shape
    rope = q_rope.shape[1] // heads
    value = wuv.shape[2]
    share = batch // t
    hc = heads // chunks
    nw, rw, vw = hc * nope, hc * rope, hc * value
    rows_in = sending.shape[0]
    pr = rows_in // n
    prefixes = plat.shape[0]
    per = n * cap

    def peer_g(d):
        return lax.rem(g + d, n)

    def peer_t(d):
        return lax.rem(y + d, t)

    loads = [pltpu.make_async_copy(a, b, load_sem.at[i]) for i, (a, b) in enumerate(zip(hbm, held))]
    for i in (0, 4, 5, 2, 3, 1):
        loads[i].start()

    barrier = pltpu.get_barrier_semaphore()

    def greet_g(d, _):
        pl.semaphore_signal(barrier, inc=1, device_id=(peer_g(d), y), device_id_type=MESH)
        return 0

    def greet_t(d, _):
        pl.semaphore_signal(barrier, inc=1, device_id=(g, peer_t(d)), device_id_type=MESH)
        return 0

    lax.fori_loop(1, n, greet_g, 0)
    lax.fori_loop(1, t, greet_t, 0)
    pl.semaphore_wait(barrier, n + t - 2)

    def rope_copy(to, at, sem):
        return pltpu.make_async_remote_copy(
            src_ref=q_rope.at[pl.ds(pl.multiple_of(to * share, share), share)],
            dst_ref=tropes.at[at],
            send_sem=rope_ss.at[sem],
            recv_sem=rope_rs.at[at],
            device_id=(g, to),
            device_id_type=MESH,
        )

    def t_copy(src, dst, ss, rs, to, at):
        return pltpu.make_async_remote_copy(
            src_ref=src, dst_ref=dst.at[at], send_sem=ss.at[to], recv_sem=rs.at[at],
            device_id=(g, to), device_id_type=MESH,
        )

    def g_copy(src, dst, ss, rs, to):
        return pltpu.make_async_remote_copy(
            src_ref=src, dst_ref=dst, send_sem=ss, recv_sem=rs,
            device_id=(to, y), device_id_type=MESH,
        )

    def each_t(fn):
        def body(d, _):
            fn(peer_t(d))
            return 0
        lax.fori_loop(1, t, body, 0)

    def each_g(fn):
        def body(d, _):
            fn(peer_g(d))
            return 0
        lax.fori_loop(1, n, body, 0)

    def q_copy(c, to, at):
        return g_copy(qs.at[c, to], qr.at[c, at], q_ss.at[c, to], q_rs.at[c, at], to)

    def v_copy(c, to, at):
        return g_copy(vbs.at[c, to], vbr.at[c, at], vb_ss.at[c, to], vb_rs.at[c, at], to)

    def s_copy(to, at):
        return g_copy(sts.at[to], strv.at[at], st_ss.at[to], st_rs.at[at], to)

    each_t(lambda to: rope_copy(to, y, to).start())

    for c in range(chunks):
        got = mm(sending[...], q_nope[:, c * nw:(c + 1) * nw]).astype(BF16)
        qs[c, :, :, :nw] = got.reshape(n, pr, nw)
        got = mm(sending[...], q_rope[:, c * rw:(c + 1) * rw]).astype(BF16)
        qs[c, :, :, nw:] = got.reshape(n, pr, rw)
        each_g(lambda to: q_copy(c, to, g).start())
        qr[c, g] = qs[c, g]

    tropes[y] = q_rope[pl.ds(pl.multiple_of(y * share, share), share), :]

    loads[0].wait()

    def own_latent(h, _):
        x = q_nope[:, pl.ds(pl.multiple_of(h * nope, nope), nope)]
        got = mm(x, wuk[h]).astype(BF16)
        qh[:, pl.ds(pl.multiple_of(h * share, share), share), :] = got.reshape(t, share, latent)
        return 0

    lax.fori_loop(0, heads, own_latent, 0, unroll=4)

    def send_latent(d, _):
        to = peer_t(d)
        tqs[to] = mm(perm[...], qh[to]).astype(BF16)
        t_copy(tqs.at[to], tqr, tq_ss, tq_rs, to, y).start()
        return 0

    lax.fori_loop(1, t, send_latent, 0)
    tqr[y] = mm(perm[...], qh[y]).astype(BF16)

    each_t(lambda at: rope_copy(at, at, at).wait_recv())

    def split_rope(s, _):
        x = tropes[s]
        stacked = jnp.concatenate([x[:, h * rope:(h + 1) * rope] for h in range(heads)], axis=0)
        rq[s] = mm(perm[...], stacked).astype(BF16)
        return 0

    lax.fori_loop(0, t, split_rope, 0)

    loads[4].wait()
    loads[5].wait()
    each_t(lambda at: t_copy(tqs.at[at], tqr, tq_ss, tq_rs, at, at).wait_recv())

    all_heads = heads * t
    slen = slat.shape[1]
    lane = lax.broadcasted_iota(jnp.int32, (all_heads, 128), 1)

    def suffix_one(r, acc):
        rows = pl.ds(pl.multiple_of(r * heads, heads), heads)
        q = tqr[:, rows, :].reshape(all_heads, latent)
        qrope = rq[:, rows, :].reshape(all_heads, rope)
        s = mm_t(q, slat[r]) + mm(qrope, srope[r])
        length = lens[y * share + r]
        live = lax.broadcasted_iota(jnp.int32, (all_heads, slen), 1) < length
        s = jnp.where(live, s, F32(-1e30))
        high = jnp.max(s, axis=1, keepdims=True)
        e = jnp.where(live, jnp.exp((s - high) * score_scale), F32(0.0))
        total = jnp.sum(e, axis=1, keepdims=True)
        o = (mm(e.astype(BF16), slat[r]) / total).astype(BF16)
        sos[:, rows, :] = o.reshape(t, heads, latent)
        acc = jnp.where(lane == r, high * score_scale, acc)
        return jnp.where(lane == share + r, total, acc)

    acc = lax.fori_loop(0, share, suffix_one, jnp.zeros((all_heads, 128), F32), unroll=4)
    ssts[...] = jnp.transpose(acc)[:2 * share, :]

    def send_suffix(to):
        t_copy(sos.at[to], sor, so_ss, so_rs, to, y).start()
        t_copy(ssts, sstr, sst_ss, sst_rs, to, y).start()

    each_t(send_suffix)
    sor[y] = sos[y]
    sstr[y] = ssts[...]

    loads[2].wait()
    loads[3].wait()
    loads[1].wait()

    st[...] = jnp.zeros_like(st)
    stat_lane = lax.broadcasted_iota(jnp.int32, (per, 128), 1)
    ht = hc // SPLIT

    def chunk(c, _):
        each_g(lambda at: q_copy(c, at, at).wait_recv())
        x = mm(sel[...], qr[c].reshape(rows_in, nw + rw)).astype(BF16)
        for p in range(prefixes):
            mine = x[p * per:(p + 1) * per]
            stats = st[p * per:(p + 1) * per, :]
            for part in range(SPLIT):
                hs = range(part * ht, (part + 1) * ht)
                q = jnp.concatenate(
                    [mm(mine[:, i * nope:(i + 1) * nope], wuk[c * hc + i]).astype(BF16) for i in hs], axis=0)
                qp = jnp.concatenate(
                    [mine[:, nw + i * rope:nw + (i + 1) * rope] for i in hs], axis=0)
                s = mm_t(q, plat[p]) + mm(qp, prope[p])
                high = jnp.max(s, axis=1, keepdims=True)
                e = jnp.exp((s - high) * score_scale)
                total = jnp.sum(e, axis=1, keepdims=True)
                o = (mm(e.astype(BF16), plat[p]) / total).astype(BF16)
                for k, i in enumerate(hs):
                    h = c * hc + i
                    block = slice(k * per, (k + 1) * per)
                    vall[p * per:(p + 1) * per, i * value:(i + 1) * value] = mm(o[block], wuv[h]).astype(BF16)
                    stats = jnp.where(stat_lane == h, high[block] * score_scale, stats)
                    stats = jnp.where(stat_lane == 64 + h, total[block], stats)
            st[p * per:(p + 1) * per, :] = stats
        vbs[c] = mm(sel_t[...], vall[...]).astype(BF16).reshape(n, pr, vw)
        each_g(lambda to: v_copy(c, to, g).start())
        vbr[c, g] = vbs[c, g]
        return 0

    lax.fori_loop(0, chunks, chunk, 0)
    sts[...] = jnp.dot(
        sel_t[...].astype(F32), st[...], precision=lax.Precision.HIGHEST, preferred_element_type=F32
    ).reshape(n, pr, 128)
    each_g(lambda to: s_copy(to, g).start())
    strv[g] = sts[g]

    def wait_suffix(at):
        t_copy(sos.at[at], sor, so_ss, so_rs, at, at).wait_recv()
        t_copy(ssts, sstr, sst_ss, sst_rs, at, at).wait_recv()

    each_t(wait_suffix)

    def unsort(s, _):
        qh[s] = mm(perm_t[...], sor[s]).astype(BF16)
        return 0

    lax.fori_loop(0, t, unsort, 0)

    def own_values(h, _):
        o = qh[:, pl.ds(pl.multiple_of(h * share, share), share), :].reshape(batch, latent)
        svals[:, pl.ds(pl.multiple_of(h * value, value), value)] = mm(o, wuv[h]).astype(BF16)
        return 0

    lax.fori_loop(0, heads, own_values, 0, unroll=4)

    each_g(lambda at: s_copy(at, at).wait_recv())
    pst = jnp.dot(
        placing[...].astype(F32), strv[...].reshape(rows_in, 128),
        precision=lax.Precision.HIGHEST, preferred_element_type=F32)
    pmax, ptotal = pst[:, :heads], pst[:, 64:64 + heads]
    sst = sstr[...]
    shift = lax.rem(128 - y * heads, 128)
    smax = pltpu.roll(sst[:, :share, :].reshape(batch, 128), shift, 1)[:, :heads]
    stotal = pltpu.roll(sst[:, share:, :].reshape(batch, 128), shift, 1)[:, :heads]
    overall = jnp.maximum(pmax, smax)
    pshare = ptotal * jnp.exp(pmax - overall)
    sshare = stotal * jnp.exp(smax - overall)
    both = pshare + sshare
    pshare = pshare / both
    sshare = sshare / both

    for c in range(chunks):
        each_g(lambda at: v_copy(c, at, at).wait_recv())
        pv = mm(placing[...], vbr[c].reshape(rows_in, vw))
        for i in range(hc):
            h = c * hc + i
            sv = svals[:, h * value:(h + 1) * value].astype(F32)
            mixed = pshare[:, h:h + 1] * pv[:, i * value:(i + 1) * value] + sshare[:, h:h + 1] * sv
            out[:, h * value:(h + 1) * value] = mixed.astype(BF16)

    each_t(lambda to: rope_copy(to, y, to).wait_send())
    each_t(lambda to: t_copy(tqs.at[to], tqr, tq_ss, tq_rs, to, y).wait_send())
    each_t(lambda to: t_copy(sos.at[to], sor, so_ss, so_rs, to, y).wait_send())
    each_t(lambda to: t_copy(ssts, sstr, sst_ss, sst_rs, to, y).wait_send())
    each_g(lambda to: s_copy(to, g).wait_send())

    def drain(c, _):
        each_g(lambda to: q_copy(c, to, g).wait_send())
        each_g(lambda to: v_copy(c, to, g).wait_send())
        return 0

    lax.fori_loop(0, chunks, drain, 0)


def local(
    q_nope, q_rope, w_uk, w_uv, prefix_latent, prefix_rope,
    suffix_latent, suffix_rope, suffix_len, request_prefix, prefix_slot,
):
    n = lax.axis_size("grp")
    t = lax.axis_size("tp")
    batch = q_nope.shape[0]
    heads, nope, latent = w_uk.shape
    value = w_uv.shape[2]
    rope = q_rope.shape[1] // heads
    prefixes = prefix_slot.shape[0]
    own = prefix_latent.shape[0]
    cap = max(2, 2 * batch // prefixes)
    pr = -(-own * cap // 16) * 16
    share = batch // t
    chunks = CHUNKS
    score_scale = 1.0 / math.sqrt(nope + rope)

    ids = jnp.arange(prefixes, dtype=jnp.int32)
    naming = (request_prefix[:, None] == ids[None, :]).astype(jnp.int32)
    slot_ids = jnp.sum(naming * prefix_slot[None, :], axis=1)
    hits = (slot_ids[:, None] == ids[None, :]).astype(jnp.int32)
    earlier = jnp.cumsum(hits, axis=0) - hits
    base = (ids // own) * pr + (ids % own) * cap
    dest = jnp.sum((earlier + base[None, :]) * hits, axis=1)
    rows = jnp.arange(n * pr, dtype=jnp.int32)
    placing = (dest[:, None] == rows[None, :]).astype(BF16)
    sending = (rows[:, None] == dest[None, :]).astype(BF16)

    i = jnp.arange(heads * share, dtype=jnp.int32)
    target = (i % heads) * share + i // heads
    perm = (target[:, None] == i[None, :]).astype(BF16)
    perm_t = (i[:, None] == target[None, :]).astype(BF16)
    k = jnp.arange(own * n * cap, dtype=jnp.int32)
    where = ((k // cap) % n) * pr + (k // (n * cap)) * cap + k % cap
    sel = (where[:, None] == rows[None, :]).astype(BF16)
    sel_t = (rows[:, None] == where[None, :]).astype(BF16)

    hc = heads // chunks
    width = hc * (nope + rope)
    vm = pl.BlockSpec(memory_space=pltpu.VMEM)
    anyspec = pl.BlockSpec(memory_space=pl.ANY)
    big = (w_uk, w_uv, prefix_latent, prefix_rope, suffix_latent, suffix_rope)
    V = pltpu.VMEM
    D = pltpu.SemaphoreType.DMA
    scratch = [V(a.shape, a.dtype) for a in big] + [
        V((chunks, n, pr, width), BF16),
        V((chunks, n, pr, width), BF16),
        V((t, heads * share, latent), BF16),
        V((t, heads * share, latent), BF16),
        V((t, heads * share, latent), BF16),
        V((t, share, heads * rope), BF16),
        V((t, heads * share, rope), BF16),
        V((t, heads * share, latent), BF16),
        V((t, heads * share, latent), BF16),
        V((2 * share, 128), F32),
        V((t, 2 * share, 128), F32),
        V((chunks, n, pr, hc * value), BF16),
        V((chunks, n, pr, hc * value), BF16),
        V((own * n * cap, 128), F32),
        V((n, pr, 128), F32),
        V((n, pr, 128), F32),
        V((own * n * cap, hc * value), BF16),
        V((batch, heads * value), BF16),
        D((6,)), D((t,)), D((t,)), D((t,)), D((t,)), D((t,)), D((t,)), D((t,)), D((t,)),
        D((chunks, n)), D((chunks, n)), D((chunks, n)), D((chunks, n)), D((n,)), D((n,)),
    ]
    return pl.pallas_call(
        functools.partial(kernel, (n, t, chunks, cap, score_scale)),
        out_shape=jax.ShapeDtypeStruct((batch, heads * value), BF16),
        in_specs=[vm] * 8 + [pl.BlockSpec(memory_space=pltpu.SMEM)] + [anyspec] * 6,
        out_specs=vm,
        scratch_shapes=scratch,
        compiler_params=pltpu.CompilerParams(
            collective_id=0, has_side_effects=True, vmem_limit_bytes=63 * 1024 * 1024),
    )(q_nope, q_rope, placing, sending, perm, perm_t, sel, sel_t, suffix_len.reshape(-1), *big)


def solution(mesh):
    in_specs = (
        P("grp", "tp"),
        P("grp", "tp"),
        P("tp", None, None),
        P("tp", None, None),
        P("grp", None, None),
        P("grp", None, None),
        P(("grp", "tp"), None, None),
        P(("grp", "tp"), None, None),
        P("grp", None),
        P("grp"),
        P(),
    )
    return jax.shard_map(local, mesh=mesh, in_specs=in_specs, out_specs=P("grp", "tp"), check_vma=False)
```

profile of v0, /device:TPU:1, one launch (start us, length us, event | category | flops | bytes accessed | tf_op | source)
XLA Modules:
  0.0 92.6 jit_solution(2105802934440210389)
XLA Ops:
  0.0 0.8 select_reduce_fusion.1
  0.9 0.1 fusion.5
  1.0 0.1 reduce_window_sum.11
  1.1 0.2 select_reduce_fusion
  1.2 0.7 fusion.6.refs_2_
  1.9 0.6 fusion.2.refs_3_
  2.5 0.7 fusion.4
  3.2 1.1 %fusion.1 = (bf16[512,512]{1,0:T(8,128)(2,1)}, bf16[512,512]{1,0:T(8,128)(2,1)}) fusion(s32[512]{0:T(512)S(1)} %fusion.11), kind=kLoop, calls=%fused_computation.3 | loop fusion | flops 1048576 | bytes 1050624 | tf_op jit(solution)/shard_map/convert_element_type | solution.py:326
  4.4 86.3 %shard_map.109 = bf16[64,4096]{1,0:T(8,128)(2,1)} custom-call(bf16[64,4096]{1,0:T(8,128)(2,1)} %refs_0_.1, bf16[64,2048]{1,0:T(8,128)(2,1)} %refs_1_.1, bf16[64,128]{1,0:T(8,128)(2,1)} %fusion.6.refs_2_, bf16[128,64]{1,0:T(8,128)(2,1)} %fusion.2.refs_3_, bf16[512,512]{1,0:T(8,128)(2,1)} %get-tuple-element.6.refs_4_, ...), custom_call_target="tpu_custom_call" | custom-call | tf_op jit(solution)/shard_map/pallas_call | solution.py:361
  90.7 1.9 %copy.13 = bf16[64,4096]{1,0:T(8,128)(2,1)} copy(bf16[64,4096]{1,0:T(8,128)(2,1)} %shard_map.109) | data formatting | bytes 1048576
  (3 shorter events, 0.0 us)
where the time goes:
time: 92.7 us; the launch traced here: 92.6 us
  Pallas kernels  86.3 us (93%)
  other arithmetic  4.33 us (5%)
  local copies, waits for them, and re-layouts  1.87 us (2%)
    pallas_call x1, Pallas kernels, local(): pl.pallas_call(functools.partial(kernel, (n, t, chunks, cap, score_scale)...  86.3 us
    unnamed x1, local copies, waits for them, and re-layouts  1.87 us

commit v1 on v0

--- a/solution.py
+++ b/solution.py
@@ -15,6 +15,26 @@
 BF16 = jnp.bfloat16
 
 
+HALVES = 2
+
+
+def quotient(x, k):
+    return x >> (k.bit_length() - 1) if k & (k - 1) == 0 else x // k
+
+
+def remainder(x, k):
+    return x & (k - 1) if k & (k - 1) == 0 else x % k
+
+
+def iotas(rows, columns):
+    shape = (rows, columns)
+    return lax.broadcasted_iota(jnp.int32, shape, 0), lax.broadcasted_iota(jnp.int32, shape, 1)
+
+
+def one_hot(x):
+    return x.astype(F32).astype(BF16)
+
+
 def mm(a, b):
     return jnp.dot(a, b, preferred_element_type=F32)
 
@@ -25,13 +45,14 @@
 
 def kernel(dims, *refs):
     n, t, chunks, cap, score_scale = dims
-    (q_nope, q_rope, placing, sending, perm, perm_t, sel, sel_t, lens) = refs[:9]
-    hbm = refs[9:15]
-    out = refs[15]
-    held = refs[16:22]
+    (q_nope, q_rope, named, slots, lens) = refs[:5]
+    hbm = refs[5:11]
+    out = refs[11]
+    held = refs[12:18]
     wuk, wuv, plat, prope, slat, srope = held
-    (qs, qr, qh, tqs, tqr, tropes, rq, sos, sor, ssts, sstr, vbs, vbr, st, sts, strv, vall, svals) = refs[22:40]
-    (load_sem, rope_ss, rope_rs, tq_ss, tq_rs, so_ss, so_rs, sst_ss, sst_rs, q_ss, q_rs, vb_ss, vb_rs, st_ss, st_rs) = refs[40:]
+    (qs, qr, qh, tqs, tqr, tropes, rq, sos, sor, ssts, sstr, vbs, vbr, st, sts, strv, vall, svals,
+     sending, perm, perm_t, sel, sel_t, acc) = refs[18:42]
+    (load_sem, rope_ss, rope_rs, tq_ss, tq_rs, so_ss, so_rs, sst_ss, sst_rs, q_ss, q_rs, vb_ss, vb_rs, st_ss, st_rs) = refs[42:]
     g = lax.axis_index("grp")
     y = lax.axis_index("tp")
     batch = q_nope.shape[0]
@@ -41,8 +62,8 @@
     share = batch // t
     hc = heads // chunks
     nw, rw, vw = hc * nope, hc * rope, hc * value
-    rows_in = sending.shape[0]
-    pr = rows_in // n
+    pr = qs.shape[2]
+    rows_in = n * pr
     prefixes = plat.shape[0]
     per = n * cap
 
@@ -86,6 +107,24 @@
             device_id=(g, to), device_id_type=MESH,
         )
 
+    half = heads * share // HALVES
+
+    def tq_copy(a, to, at):
+        rows = pl.ds(pl.multiple_of(a * half, half), half)
+        return pltpu.make_async_remote_copy(
+            src_ref=tqs.at[to, rows], dst_ref=tqr.at[at, rows],
+            send_sem=tq_ss.at[a, to], recv_sem=tq_rs.at[a, at],
+            device_id=(g, to), device_id_type=MESH,
+        )
+
+    def so_copy(a, to, at):
+        rows = pl.ds(pl.multiple_of(a * half, half), half)
+        return pltpu.make_async_remote_copy(
+            src_ref=sos.at[to, rows], dst_ref=sor.at[at, rows],
+            send_sem=so_ss.at[a, to], recv_sem=so_rs.at[a, at],
+            device_id=(g, to), device_id_type=MESH,
+        )
+
     def g_copy(src, dst, ss, rs, to):
         return pltpu.make_async_remote_copy(
             src_ref=src, dst_ref=dst, send_sem=ss, recv_sem=rs,
@@ -115,13 +154,39 @@
 
     each_t(lambda to: rope_copy(to, y, to).start())
 
+    who = named[...]
+    slot = jnp.zeros_like(who)
+    for k in range(n * prefixes):
+        slot = jnp.where(who == k, slots[0, k], slot)
+    row, _ = iotas(n * prefixes, batch)
+    hits = (row == slot).astype(F32)
+    first, second = iotas(batch, batch)
+    earlier = mm(hits.astype(BF16), one_hot(first < second))
+    base = quotient(row, prefixes) * pr + remainder(row, prefixes) * cap
+    dest = jnp.sum(hits * (earlier + base.astype(F32)), axis=0, keepdims=True).astype(jnp.int32)
+    row, _ = iotas(rows_in, batch)
+    sending[...] = (row == dest).astype(F32)
+    send_hot = sending[...].astype(BF16)
+
     for c in range(chunks):
-        got = mm(sending[...], q_nope[:, c * nw:(c + 1) * nw]).astype(BF16)
+        got = mm(send_hot, q_nope[:, c * nw:(c + 1) * nw]).astype(BF16)
         qs[c, :, :, :nw] = got.reshape(n, pr, nw)
-        got = mm(sending[...], q_rope[:, c * rw:(c + 1) * rw]).astype(BF16)
+        got = mm(send_hot, q_rope[:, c * rw:(c + 1) * rw]).astype(BF16)
         qs[c, :, :, nw:] = got.reshape(n, pr, rw)
         each_g(lambda to: q_copy(c, to, g).start())
         qr[c, g] = qs[c, g]
+
+    i, j = iotas(heads * share, heads * share)
+    perm[...] = one_hot(j == remainder(i, heads) * share + quotient(i, heads))
+    perm_t[...] = one_hot(i == remainder(j, heads) * share + quotient(j, heads))
+
+    def place(k):
+        return remainder(quotient(k, cap), n) * pr + quotient(k, n * cap) * cap + remainder(k, cap)
+
+    i, j = iotas(prefixes * per, rows_in)
+    sel[...] = one_hot(place(i) == j)
+    i, j = iotas(rows_in, prefixes * per)
+    sel_t[...] = one_hot(place(j) == i)
 
     tropes[y] = q_rope[pl.ds(pl.multiple_of(y * share, share), share), :]
 
@@ -135,16 +200,17 @@
 
     lax.fori_loop(0, heads, own_latent, 0, unroll=4)
 
-    def send_latent(d, _):
-        to = peer_t(d)
-        tqs[to] = mm(perm[...], qh[to]).astype(BF16)
-        t_copy(tqs.at[to], tqr, tq_ss, tq_rs, to, y).start()
-        return 0
-
-    lax.fori_loop(1, t, send_latent, 0)
+    for a in range(HALVES):
+        def send_latent(to):
+            tqs[to, a * half:(a + 1) * half] = mm(perm[a * half:(a + 1) * half, :], qh[to]).astype(BF16)
+            tq_copy(a, to, y).start()
+
+        each_t(send_latent)
     tqr[y] = mm(perm[...], qh[y]).astype(BF16)
 
-    each_t(lambda at: rope_copy(at, at, at).wait_recv())
+    all_heads = heads * t
+    slen = slat.shape[1]
+    lane = lax.broadcasted_iota(jnp.int32, (all_heads, 128), 1)
 
     def split_rope(s, _):
         x = tropes[s]
@@ -152,22 +218,12 @@
         rq[s] = mm(perm[...], stacked).astype(BF16)
         return 0
 
-    lax.fori_loop(0, t, split_rope, 0)
-
-    loads[4].wait()
-    loads[5].wait()
-    each_t(lambda at: t_copy(tqs.at[at], tqr, tq_ss, tq_rs, at, at).wait_recv())
-
-    all_heads = heads * t
-    slen = slat.shape[1]
-    lane = lax.broadcasted_iota(jnp.int32, (all_heads, 128), 1)
-
-    def suffix_one(r, acc):
+    def suffix_one(r, _):
         rows = pl.ds(pl.multiple_of(r * heads, heads), heads)
         q = tqr[:, rows, :].reshape(all_heads, latent)
         qrope = rq[:, rows, :].reshape(all_heads, rope)
         s = mm_t(q, slat[r]) + mm(qrope, srope[r])
-        length = lens[y * share + r]
+        length = lens[0, y * share + r]
         live = lax.broadcasted_iota(jnp.int32, (all_heads, slen), 1) < length
         s = jnp.where(live, s, F32(-1e30))
         high = jnp.max(s, axis=1, keepdims=True)
@@ -175,19 +231,36 @@
         total = jnp.sum(e, axis=1, keepdims=True)
         o = (mm(e.astype(BF16), slat[r]) / total).astype(BF16)
         sos[:, rows, :] = o.reshape(t, heads, latent)
-        acc = jnp.where(lane == r, high * score_scale, acc)
-        return jnp.where(lane == share + r, total, acc)
-
-    acc = lax.fori_loop(0, share, suffix_one, jnp.zeros((all_heads, 128), F32), unroll=4)
-    ssts[...] = jnp.transpose(acc)[:2 * share, :]
-
-    def send_suffix(to):
-        t_copy(sos.at[to], sor, so_ss, so_rs, to, y).start()
-        t_copy(ssts, sstr, sst_ss, sst_rs, to, y).start()
-
-    each_t(send_suffix)
-    sor[y] = sos[y]
-    sstr[y] = ssts[...]
+        stats = jnp.where(lane == r, high * score_scale, acc[...])
+        acc[...] = jnp.where(lane == share + r, total, stats)
+        return 0
+
+    def suffix_half(a):
+        @pl.when(a == 0)
+        def _():
+            each_t(lambda at: rope_copy(at, at, at).wait_recv())
+            lax.fori_loop(0, t, split_rope, 0)
+            loads[4].wait()
+            loads[5].wait()
+            acc[...] = jnp.zeros_like(acc)
+
+        each_t(lambda at: tq_copy(a, at, at).wait_recv())
+        some = share // HALVES
+
+        def two(k, _):
+            for u in range(2):
+                suffix_one(a * some + k * 2 + u, 0)
+            return 0
+
+        lax.fori_loop(0, some // 2, two, 0)
+        each_t(lambda to: so_copy(a, to, y).start())
+
+        @pl.when(a == HALVES - 1)
+        def _():
+            ssts[...] = jnp.transpose(acc[...])[:2 * share, :]
+            each_t(lambda to: t_copy(ssts, sstr, sst_ss, sst_rs, to, y).start())
+            sor[y] = sos[y]
+            sstr[y] = ssts[...]
 
     loads[2].wait()
     loads[3].wait()
@@ -221,20 +294,28 @@
                     stats = jnp.where(stat_lane == h, high[block] * score_scale, stats)
                     stats = jnp.where(stat_lane == 64 + h, total[block], stats)
             st[p * per:(p + 1) * per, :] = stats
+        @pl.when(c == chunks - 1)
+        def _():
+            sts[...] = jnp.dot(
+                sel_t[...].astype(F32), st[...], precision=lax.Precision.HIGHEST, preferred_element_type=F32
+            ).reshape(n, pr, 128)
+            each_g(lambda to: s_copy(to, g).start())
+            strv[g] = sts[g]
+
         vbs[c] = mm(sel_t[...], vall[...]).astype(BF16).reshape(n, pr, vw)
         each_g(lambda to: v_copy(c, to, g).start())
         vbr[c, g] = vbs[c, g]
+
+        @pl.when(c < HALVES)
+        def _():
+            suffix_half(c)
+
         return 0
 
     lax.fori_loop(0, chunks, chunk, 0)
-    sts[...] = jnp.dot(
-        sel_t[...].astype(F32), st[...], precision=lax.Precision.HIGHEST, preferred_element_type=F32
-    ).reshape(n, pr, 128)
-    each_g(lambda to: s_copy(to, g).start())
-    strv[g] = sts[g]
-
     def wait_suffix(at):
-        t_copy(sos.at[at], sor, so_ss, so_rs, at, at).wait_recv()
+        for a in range(HALVES):
+            so_copy(a, at, at).wait_recv()
         t_copy(ssts, sstr, sst_ss, sst_rs, at, at).wait_recv()
 
     each_t(wait_suffix)
@@ -253,8 +334,10 @@
     lax.fori_loop(0, heads, own_values, 0, unroll=4)
 
     each_g(lambda at: s_copy(at, at).wait_recv())
+    placed = jnp.transpose(sending[...])
+    placing = placed.astype(BF16)
     pst = jnp.dot(
-        placing[...].astype(F32), strv[...].reshape(rows_in, 128),
+        placed, strv[...].reshape(rows_in, 128),
         precision=lax.Precision.HIGHEST, preferred_element_type=F32)
     pmax, ptotal = pst[:, :heads], pst[:, 64:64 + heads]
     sst = sstr[...]
@@ -270,7 +353,7 @@
 
     for c in range(chunks):
         each_g(lambda at: v_copy(c, at, at).wait_recv())
-        pv = mm(placing[...], vbr[c].reshape(rows_in, vw))
+        pv = mm(placing, vbr[c].reshape(rows_in, vw))
         for i in range(hc):
             h = c * hc + i
             sv = svals[:, h * value:(h + 1) * value].astype(F32)
@@ -278,8 +361,9 @@
             out[:, h * value:(h + 1) * value] = mixed.astype(BF16)
 
     each_t(lambda to: rope_copy(to, y, to).wait_send())
-    each_t(lambda to: t_copy(tqs.at[to], tqr, tq_ss, tq_rs, to, y).wait_send())
-    each_t(lambda to: t_copy(sos.at[to], sor, so_ss, so_rs, to, y).wait_send())
+    for a in range(HALVES):
+        each_t(lambda to: tq_copy(a, to, y).wait_send())
+        each_t(lambda to: so_copy(a, to, y).wait_send())
     each_t(lambda to: t_copy(ssts, sstr, sst_ss, sst_rs, to, y).wait_send())
     each_g(lambda to: s_copy(to, g).wait_send())
 
@@ -308,26 +392,6 @@
     share = batch // t
     chunks = CHUNKS
     score_scale = 1.0 / math.sqrt(nope + rope)
-
-    ids = jnp.arange(prefixes, dtype=jnp.int32)
-    naming = (request_prefix[:, None] == ids[None, :]).astype(jnp.int32)
-    slot_ids = jnp.sum(naming * prefix_slot[None, :], axis=1)
-    hits = (slot_ids[:, None] == ids[None, :]).astype(jnp.int32)
-    earlier = jnp.cumsum(hits, axis=0) - hits
-    base = (ids // own) * pr + (ids % own) * cap
-    dest = jnp.sum((earlier + base[None, :]) * hits, axis=1)
-    rows = jnp.arange(n * pr, dtype=jnp.int32)
-    placing = (dest[:, None] == rows[None, :]).astype(BF16)
-    sending = (rows[:, None] == dest[None, :]).astype(BF16)
-
-    i = jnp.arange(heads * share, dtype=jnp.int32)
-    target = (i % heads) * share + i // heads
-    perm = (target[:, None] == i[None, :]).astype(BF16)
-    perm_t = (i[:, None] == target[None, :]).astype(BF16)
-    k = jnp.arange(own * n * cap, dtype=jnp.int32)
-    where = ((k // cap) % n) * pr + (k // (n * cap)) * cap + k % cap
-    sel = (where[:, None] == rows[None, :]).astype(BF16)
-    sel_t = (rows[:, None] == where[None, :]).astype(BF16)
 
     hc = heads // chunks
     width = hc * (nope + rope)
@@ -355,18 +419,24 @@
         V((n, pr, 128), F32),
         V((own * n * cap, hc * value), BF16),
         V((batch, heads * value), BF16),
-        D((6,)), D((t,)), D((t,)), D((t,)), D((t,)), D((t,)), D((t,)), D((t,)), D((t,)),
+        V((n * pr, batch), F32),
+        V((heads * share, heads * share), BF16),
+        V((heads * share, heads * share), BF16),
+        V((own * n * cap, n * pr), BF16),
+        V((n * pr, own * n * cap), BF16),
+        V((heads * t, 128), F32),
+        D((6,)), D((t,)), D((t,)), D((HALVES, t)), D((HALVES, t)), D((HALVES, t)), D((HALVES, t)), D((t,)), D((t,)),
         D((chunks, n)), D((chunks, n)), D((chunks, n)), D((chunks, n)), D((n,)), D((n,)),
     ]
     return pl.pallas_call(
         functools.partial(kernel, (n, t, chunks, cap, score_scale)),
         out_shape=jax.ShapeDtypeStruct((batch, heads * value), BF16),
-        in_specs=[vm] * 8 + [pl.BlockSpec(memory_space=pltpu.SMEM)] + [anyspec] * 6,
+        in_specs=[vm] * 3 + [pl.BlockSpec(memory_space=pltpu.SMEM)] * 2 + [anyspec] * 6,
         out_specs=vm,
         scratch_shapes=scratch,
         compiler_params=pltpu.CompilerParams(
             collective_id=0, has_side_effects=True, vmem_limit_bytes=63 * 1024 * 1024),
-    )(q_nope, q_rope, placing, sending, perm, perm_t, sel, sel_t, suffix_len.reshape(-1), *big)
+    )(q_nope, q_rope, request_prefix.reshape(1, -1), prefix_slot.reshape(1, -1), suffix_len, *big)
 
 
 def solution(mesh):

time: 92.7 us -> 77.7 us (0.84)
  the two profiles are of different devices: /device:TPU:1 before, /device:TPU:0 now
where the time goes in v1:
time: 77.7 us; the launch traced here: 77.5 us
  Pallas kernels  75.7 us (97%)
  local copies, waits for them, and re-layouts  1.87 us (2%)
    pallas_call x1, Pallas kernels, local(): pl.pallas_call(functools.partial(kernel, (n, t, chunks, cap, score_scale)...  75.7 us
    unnamed x1, local copies, waits for them, and re-layouts  1.87 us

profile of v1, /device:TPU:0, one launch (start us, length us, event | category | flops | bytes accessed | tf_op | source)
XLA Modules:
  0.0 77.5 jit_solution(6036344203910049645)
XLA Ops:
  0.0 75.7 %shard_map.109 = bf16[64,4096]{1,0:T(8,128)(2,1)} custom-call(bf16[64,4096]{1,0:T(8,128)(2,1)} %refs_0_.1, bf16[64,2048]{1,0:T(8,128)(2,1)} %refs_1_.1, s32[1,64]{1,0:T(1,128)} %bitcast.2, s32[1,16]{1,0:T(1,128)} %bitcast.3, s32[1,64]{1,0:T(1,128)} %refs_4_.1, bf16[32,128,512]{2,1,0:T(8,128)(2,1)} %refs_5_.1, bf16[32,512,128]{2,1,0:T(8,128)(2,1)} %refs_6_.1, ...), custom_call_target="tpu_custom_call" | custom-call | tf_op jit(solution)/shard_map/pallas_call | solution.py:431
  75.7 1.9 %copy.13 = bf16[64,4096]{1,0:T(8,128)(2,1)} copy(bf16[64,4096]{1,0:T(8,128)(2,1)} %shard_map.109) | data formatting | bytes 1048576

commit v2 on v1

--- a/solution.py
+++ b/solution.py
@@ -9,13 +9,14 @@
 from jax.sharding import PartitionSpec as P
 
 MESH = pl.DeviceIdType.MESH
-CHUNKS = 4
-SPLIT = 2
+CHUNKS = 8
+SPLIT = 1
 F32 = jnp.float32
 BF16 = jnp.bfloat16
 
 
 HALVES = 2
+SUFFIX_AT = (2, 4)
 
 
 def quotient(x, k):
@@ -236,8 +237,7 @@
         return 0
 
     def suffix_half(a):
-        @pl.when(a == 0)
-        def _():
+        if a == 0:
             each_t(lambda at: rope_copy(at, at, at).wait_recv())
             lax.fori_loop(0, t, split_rope, 0)
             loads[4].wait()
@@ -255,8 +255,7 @@
         lax.fori_loop(0, some // 2, two, 0)
         each_t(lambda to: so_copy(a, to, y).start())
 
-        @pl.when(a == HALVES - 1)
-        def _():
+        if a == HALVES - 1:
             ssts[...] = jnp.transpose(acc[...])[:2 * share, :]
             each_t(lambda to: t_copy(ssts, sstr, sst_ss, sst_rs, to, y).start())
             sor[y] = sos[y]
@@ -306,9 +305,10 @@
         each_g(lambda to: v_copy(c, to, g).start())
         vbr[c, g] = vbs[c, g]
 
-        @pl.when(c < HALVES)
-        def _():
-            suffix_half(c)
+        for a, at in enumerate(SUFFIX_AT):
+            @pl.when(c == at)
+            def _():
+                suffix_half(a)
 
         return 0
 

time: 77.7 us -> 79.6 us (1.024)
  Pallas kernels: 75.7 us -> 77.6 us
    pallas_call x1, Pallas kernels: 75.7 us -> 77.6 us  [local(): pl.pallas_call(functools.partial(kernel, (n, t, chunks, cap, score_scale)...]
where the time goes in v2:
time: 79.6 us; the launch traced here: 79.4 us
  Pallas kernels  77.6 us (97%)
  local copies, waits for them, and re-layouts  1.87 us (2%)
    pallas_call x1, Pallas kernels, local(): pl.pallas_call(functools.partial(kernel, (n, t, chunks, cap, score_scale)...  77.6 us
    unnamed x1, local copies, waits for them, and re-layouts  1.87 us

profile of v2, /device:TPU:0, one launch (start us, length us, event | category | flops | bytes accessed | tf_op | source)
XLA Modules:
  0.0 79.4 jit_solution(6586120503197134395)
XLA Ops:
  0.0 77.6 %shard_map.109 = bf16[64,4096]{1,0:T(8,128)(2,1)} custom-call(bf16[64,4096]{1,0:T(8,128)(2,1)} %refs_0_.1, bf16[64,2048]{1,0:T(8,128)(2,1)} %refs_1_.1, s32[1,64]{1,0:T(1,128)} %bitcast.2, s32[1,16]{1,0:T(1,128)} %bitcast.3, s32[1,64]{1,0:T(1,128)} %refs_4_.1, bf16[32,128,512]{2,1,0:T(8,128)(2,1)} %refs_5_.1, bf16[32,512,128]{2,1,0:T(8,128)(2,1)} %refs_6_.1, ...), custom_call_target="tpu_custom_call" | custom-call | tf_op jit(solution)/shard_map/pallas_call | solution.py:431
  77.6 1.9 %copy.13 = bf16[64,4096]{1,0:T(8,128)(2,1)} copy(bf16[64,4096]{1,0:T(8,128)(2,1)} %shard_map.109) | data formatting | bytes 1048576
